TPU v7x, 32 devices: a whole 2x2x4 slice. The times are simulated.
32 devices in a mesh: lat: 8 (over y, x, core), lon: 4 (over z).
Axes of the slice: x: 2, y: 2, z: 4, core: 2. Of those that a mesh axis runs over, the one named last changes fastest.
Arguments:
- coeffs_old: float32 [640, 2, 3, 50, 640], P(('lat', 'lon')), may hold values from -0.16 to 0.16
- noise: bfloat16 [640, 2, 3, 50, 640], P(('lat', 'lon')), may hold values from -6 to 6
- legendre: float32 [640, 640, 640], P(('lat', 'lon')), may hold values from -0.25 to 0.25
- decay: float32 [3], replicated, may hold values from 0.3 to 0.97
- amplitude: float32 [3, 640], replicated, may hold values from 0.005 to 0.05
- wavenumber_of_slot: int32 [640], replicated, may hold values from 0 to 639, as said below
- lat_order: int32 [640], replicated, may hold values from 0 to 639, each once
Outputs:
- coeffs_new: float32 [640, 2, 3, 50, 640], P(('lat', 'lon'))
- pattern: float32 [640, 50, 1280], P(('lat', 'lon'))
Inputs may be any that keep to these rules, and one draw needn't show every extreme that they name: `wavenumber_of_slot`: every wavenumber fills exactly one slot; the sums of the wavenumbers of one device's 20 slots differ between devices by less than 32. `lat_order`: every latitude stands in exactly one row.
All inputs are finite; a program needn't handle non-finite values.
Results may differ from a plain program's by a relative error of at most 0.0003.
Values sent between devices are 32-bit elements; how exact they have to be, the bound alone decides.
A program may use at most 192 MiB of HBM per device.

v0:
```python
import jax
import jax.numpy as jnp
from jax import lax
from jax.sharding import PartitionSpec as P

LON = 1280
TWO_PI = 6.283185307179586


def evolve(coeffs_old, noise, decay, amplitude, waves):
    width = coeffs_old.shape[4]
    offsets = lax.broadcasted_iota(jnp.int32, (waves.shape[0], width), 1)
    live = waves[:, None] + offsets < width
    padded = jnp.concatenate([amplitude, jnp.zeros_like(amplitude)], axis=1)
    spread = jax.vmap(lambda wave: lax.dynamic_slice_in_dim(padded, wave, width, 1))(waves)
    factor = jnp.sqrt(1.0 - decay * decay)
    fresh = decay[None, None, :, None, None] * coeffs_old + (spread * factor[None, :, None])[
        :, None, :, None, :
    ] * noise.astype(jnp.float32)
    return jnp.where(live[:, None, None, None, :], fresh, jnp.zeros_like(fresh))


def synthesis_table(waves, length):
    column = lax.broadcasted_iota(jnp.int32, (waves.shape[0], length), 1)
    phase = waves[:, None] * column % length
    angle = phase.astype(jnp.float32) * (TWO_PI / length)
    weight = jnp.where(waves == 0, 1.0, 2.0).astype(jnp.float32)[:, None]
    return jnp.stack([weight * jnp.cos(angle), -weight * jnp.sin(angle)], axis=1)


def synthesize(values, table):
    return jnp.einsum("sreq,srl->qel", values, table, precision=lax.Precision.HIGHEST)


def local(coeffs_old, noise, legendre, decay, amplitude, wavenumber_of_slot, lat_order):
    lat_count = lax.axis_size("lat")
    lon_count = lax.axis_size("lon")
    lat_index = lax.axis_index("lat")
    lon_index = lax.axis_index("lon")
    slots = coeffs_old.shape[0]
    mine = lax.dynamic_slice_in_dim(
        wavenumber_of_slot, (lat_index * lon_count + lon_index) * slots, slots
    )
    coeffs_new = evolve(coeffs_old, noise, decay, amplitude, mine)
    field = jnp.einsum("srkej,slj->srel", coeffs_new, legendre, precision=lax.Precision.HIGHEST)
    field = jnp.take(field, lat_order, axis=3)
    ordered = wavenumber_of_slot.reshape(lat_count, lon_count, slots).transpose(1, 0, 2).reshape(-1)
    full_table = synthesis_table(ordered, LON)
    pattern = synthesize(
        lax.all_to_all(
            lax.all_to_all(field, "lat", split_axis=3, concat_axis=0, tiled=True),
            "lon",
            split_axis=3,
            concat_axis=0,
            tiled=True,
        ),
        full_table,
    )
    return (coeffs_new, pattern)


def solution(mesh):
    in_specs = (
        P(("lat", "lon"), None, None, None, None),
        P(("lat", "lon"), None, None, None, None),
        P(("lat", "lon"), None, None),
        P(),
        P(),
        P(),
        P(),
    )
    out_specs = (P(("lat", "lon"), None, None, None, None), P(("lat", "lon"), None, None))
    return jax.shard_map(local, mesh=mesh, in_specs=in_specs, out_specs=out_specs, check_vma=False)
```

profile of v0, /device:TPU:0, one launch (start us, length us, event | category | flops | bytes accessed | tf_op | source)
XLA Modules:
  0.0 590.6 jit_solution(11389839738425668350)
XLA Ops:
  2.0 0.8 fusion.12
  3.5 26.4 %while.1 = (s32[]{:T(128)}, f32[3,1280]{1,0:T(4,128)S(1)}, s32[20,2]{0,1:T(2,128)S(1)}, f32[20,3,640]{2,1,0:T(4,128)S(1)}, s32[]{:T(128)}) while((s32[]{:T(128)}, f32[3,1280]{1,0:T(4,128)S(1)}, s32[20,2]{0,1:T(2,128)S(1)}, f32[20,3,640]{2,1,0:T(4,128)S(1)}, s32[]{:T(128)}) %tuple.24), condition=%wide.while_cond, body=%wide.while_body.sunk | while | flops 2 | bytes 20585 | solution.py:15
  4.1 0.7 bitcast_dynamic-update-slice_fusion.2
  5.4 0.7 bitcast_dynamic-update-slice_fusion.2
  6.7 0.7 bitcast_dynamic-update-slice_fusion.2
  8.1 0.7 bitcast_dynamic-update-slice_fusion.2
  9.4 0.7 bitcast_dynamic-update-slice_fusion.2
  10.7 0.7 bitcast_dynamic-update-slice_fusion.2
  12.0 0.7 bitcast_dynamic-update-slice_fusion.2
  13.3 0.7 bitcast_dynamic-update-slice_fusion.2
  14.7 0.7 bitcast_dynamic-update-slice_fusion.2
  16.0 0.7 bitcast_dynamic-update-slice_fusion.2
  17.3 0.7 bitcast_dynamic-update-slice_fusion.2
  18.6 0.7 bitcast_dynamic-update-slice_fusion.2
  30.8 32.2 %fusion.15 = (f32[20,2,50,640]{3,1,2,0:T(2,128)}, f32[20,2,3,50,640]{4,1,3,2,0:T(2,128)}) fusion(bf16[20,2,3,50,640]{4,1,3,2,0:T(2,128)(2,1)} %param.8, f32[20,3,640]{2,1,0:T(4,128)S(1)} %broadcast_multiply_fusion, f32[20,2,3,50,640]{4,1,3,2,0:T(2,128)} %param.7, f32[3]{0:T(128)} %param.10, pred[20,640]{1,0:T(8,128)(4,1)S(1)} %add_compare_fusion), kind=kLoop, calls=%fused_computation.33 | loop fusion | flops 21760000 | bytes 43686412 | tf_op jit(solution)/shard_map/srkej,slj->srel/reduce_sum | solution.py:45
  63.0 36.1 %fusion = f32[20,2,50,640]{3,2,1,0:T(8,128)} fusion(f32[20,640,640]{2,1,0:T(8,128)} %param.9, f32[20,2,50,640]{3,1,2,0:T(2,128)} %get-tuple-element.18), kind=kOutput, calls=%fused_computation.3 | convolution fusion | flops 9830400000 | bytes 43008000 | tf_op jit(solution)/shard_map/srkej,slj->srel/dot_general | solution.py:45
  99.1 15.9 %copy.33 = f32[20,2,50,640]{2,1,3,0:T(2,128)} copy(f32[20,2,50,640]{3,2,1,0:T(8,128)} %fusion) | data formatting | bytes 10240000 | tf_op jit(solution)/shard_map/srkej,slj->srel/dot_general | solution.py:45
  115.0 38.6 %gather_fusion = f32[640,20,2,50]{3,2,1,0:T(2,128)} fusion(f32[20,2,50,640]{2,1,3,0:T(2,128)} %copy.33, s32[1024]{0:T(1024)S(1)} %pad_clamp_fusion), kind=kCustom, calls=%fused_computation | custom fusion | bytes 10242560 | tf_op jit(solution)/shard_map/jit(_take)/gather | solution.py:46
  153.6 10.2 %fusion.16 = f32[640,20,2,50]{3,2,1,0:T(2,128)} fusion(f32[640,20,2,50]{3,2,1,0:T(2,128)} %gather_fusion, pred[640]{0:T(1024)(128)(4,1)S(1)} %compare_and_fusion), kind=kLoop, calls=%fused_computation.34 | loop fusion | flops 1280000 | bytes 10240640
  163.8 27.8 %reshape.218 = f32[8,1,160000]{2,1,0:T(1,128)} reshape(f32[640,20,2,50]{3,2,1,0:T(2,128)} %fusion.16) | data formatting | bytes 10240000
  191.5 64.3 %all_to_all.36 = f32[8,1,160000]{2,1,0:T(1,128)} all-to-all(f32[8,1,160000]{2,1,0:T(1,128)} %reshape.218), channel_id=1, replica_groups=mesh['lat'=8,'lon'=4] {'lat'}, dimensions={0} | all-to-all | bytes 10240000 | tf_op jit(solution)/shard_map/all_to_all | solution.py:51
  256.3 17.0 %reduce = f32[8,160000]{1,0:T(8,128)} reduce(f32[8,1,160000]{2,1,0:T(1,128)} %all_to_all.36, f32[]{:T(128)} %broadcast.203), dimensions={1}, to_apply=%all_to_all.26.reduce_sub_computation | reduce | bytes 10240004 | tf_op jit(solution)/shard_map/all_to_all | solution.py:51
  273.3 33.3 %reshape.219 = f32[640,20,2,50]{3,2,1,0:T(2,128)} reshape(f32[8,160000]{1,0:T(8,128)} %reduce) | data formatting | bytes 10240000
  306.6 17.1 %copy.42 = f32[20,2,50,8,80]{4,3,1,2,0:T(8,128)} copy(f32[20,2,50,8,80]{2,1,0,4,3:T(2,128)} %bitcast.41) | data formatting | bytes 10240000 | tf_op jit(solution)/shard_map/all_to_all | solution.py:51
  323.7 13.0 %copy.35 = f32[8,20,2,50,80]{4,2,3,1,0:T(2,128)} copy(f32[8,20,2,50,80]{4,0,2,3,1:T(8,128)} %bitcast.43) | data formatting | bytes 10240000 | tf_op jit(solution)/shard_map/all_to_all | solution.py:51
  336.7 18.0 %copy.36 = f32[160,2,50,80]{0,1,2,3:T(2,128)} copy(f32[160,2,50,80]{3,1,2,0:T(2,128)} %bitcast.42) | data formatting | bytes 10240000 | tf_op jit(solution)/shard_map/all_to_all | solution.py:51
  354.7 5.7 all-to-all-start.1
  360.7 15.2 %cosine_multiply_fusion = (f32[640,1,1280]{2,0,1:T(8,128)S(1)}, f32[640,1,1280]{2,0,1:T(8,128)}) fusion(s32[640]{0:T(1024)S(1)} %reshape.185, f32[640]{0:T(1024)S(1)} %get-tuple-element.24, f32[640]{0:T(1024)S(1)} %get-tuple-element.25), kind=kLoop, calls=%fused_computation.17 | loop fusion | flops 9011200 | bytes 6561280 | tf_op jit(solution)/shard_map/mul | solution.py:28
  375.9 164.0 %all-to-all-done.1 = f32[160,2,50,80]{0,1,2,3:T(2,128)} async-done(((f32[160,2,50,80]{0,1,2,3:T(2,128)}), f32[160,2,50,80]{0,1,2,3:T(2,128)}, u32[]{:S(2)}, u32[]{:S(2)}) %all-to-all-start.1) | async-done | bytes 5120032 | tf_op jit(solution)/shard_map/all_to_all | solution.py:50
  539.9 11.8 %copy.44 = f32[4,160,2,50,20]{1,0,3,2,4:T(4,128)} copy(f32[4,160,2,50,20]{1,2,3,4,0:T(2,128)} %bitcast.11) | data formatting | bytes 10240000 | tf_op jit(solution)/shard_map/all_to_all | solution.py:50
  551.7 9.5 %reshape.217 = f32[640,2,50,20]{0,2,1,3:T(8,128)} reshape(f32[4,160,2,50,20]{1,0,3,2,4:T(4,128)} %copy.44) | data formatting | bytes 10240000 | tf_op jit(solution)/shard_map/all_to_all | solution.py:50
  561.3 29.1 %fusion.6 = f32[20,50,1280]{2,1,0:T(8,128)} fusion(f32[640,2,50,20]{0,2,1,3:T(8,128)} %reshape.217, f32[640,1,1280]{2,0,1:T(8,128)} %get-tuple-element.23, f32[640,1,1280]{2,0,1:T(8,128)S(1)} %get-tuple-element.22), kind=kOutput, calls=%fused_computation.13 | convolution fusion | flops 19662438400 | bytes 16793600 | tf_op jit(solution)/shard_map/sreq,srl->qel/dot_general | solution.py:32
  (64 shorter events, 21.3 us)
Async XLA Ops:
  354.7 5.8 copy-start
  354.7 185.2 %all-to-all-start.1 = ((f32[160,2,50,80]{0,1,2,3:T(2,128)}), f32[160,2,50,80]{0,1,2,3:T(2,128)}, u32[]{:S(2)}, u32[]{:S(2)}) async-start(f32[160,2,50,80]{0,1,2,3:T(2,128)} %copy.36), calls=%async_computation.1 | async-start | bytes 16384000 | tf_op jit(solution)/shard_map/all_to_all | solution.py:50
where the time goes:
time: 601 us; the launch traced here: 591 us
  local copies, waits for them, and re-layouts  213 us (35%)
  waiting for transfers between devices  164 us (27%)
  other arithmetic  77.6 us (13%)
  matrix products  65.2 us (11%)
  blocking collectives  64.3 us (11%)
    all_to_all x1, waiting for transfers between devices, local(): lax.all_to_all(lax.all_to_all(field, 'lat', split_axis=3, concat_axis=0,...  164 us
    all_to_all x1, blocking collectives, local(): lax.all_to_all(field, 'lat', split_axis=3, concat_axis=0, tiled=True)  64.3 us
    unnamed x4, local copies, waits for them, and re-layouts  61.1 us
    all_to_all x4, local copies, waits for them, and re-layouts, local(): lax.all_to_all(field, 'lat', split_axis=3, concat_axis=0, tiled=True)  48.6 us
    gather x1, local copies, waits for them, and re-layouts, local(): field = jnp.take(field, lat_order, axis=3)  38.6 us
    dot_general x1, matrix products, local(): jnp.einsum('srkej,slj->srel', coeffs_new, legendre, precision=lax.Precisi...  36.1 us
    reduce_sum x1, other arithmetic, local(): jnp.einsum('srkej,slj->srel', coeffs_new, legendre, precision=lax.Precisi...  32.2 us
    dot_general x1, matrix products, synthesize(): jnp.einsum('sreq,srl->qel', values, table, precision=lax.Precision.HIGHEST)  29.1 us
  transfers between devices with their start and end apart: 1, of which 1 were waited for; matrix products, arithmetic and copies ran while one was open for 3% of the time, Pallas kernels for 0%

commit v1 on v0

--- a/solution.py
+++ b/solution.py
@@ -5,6 +5,13 @@
 
 LON = 1280
 TWO_PI = 6.283185307179586
+
+
+def swap_blocks(x, name, split, join):
+    count = lax.axis_size(name)
+    tiles = jnp.stack(jnp.split(x, count, axis=split), axis=0)
+    tiles = lax.all_to_all(tiles, name, split_axis=0, concat_axis=0)
+    return jnp.concatenate(tiles, axis=join)
 
 
 def evolve(coeffs_old, noise, decay, amplitude, waves):
@@ -48,11 +55,7 @@
     full_table = synthesis_table(ordered, LON)
     pattern = synthesize(
         lax.all_to_all(
-            lax.all_to_all(field, "lat", split_axis=3, concat_axis=0, tiled=True),
-            "lon",
-            split_axis=3,
-            concat_axis=0,
-            tiled=True,
+            swap_blocks(field, "lat", 3, 0), "lon", split_axis=3, concat_axis=0, tiled=True
         ),
         full_table,
     )

time: 601 us -> 551 us (0.917); the launches traced: 591 us -> 548 us
  local copies, waits for them, and re-layouts: 213 us -> 154 us
  blocking collectives: 64.3 us -> 98.3 us
  other arithmetic: 77.6 us -> 59.6 us
    unnamed x4 -> x9, local copies, waits for them, and re-layouts: 61.1 us -> 9.09 us
    all_to_all x6 -> x2, local copies, waits for them, and re-layouts: 69.9 us -> 21.3 us  [local(): lax.all_to_all(swap_blocks(field, 'lat', 3, 0), 'lon', split_axis=3, conc...]
    all_to_all x1, blocking collectives: 64.3 us -> 98.3 us  [swap_blocks(): tiles = lax.all_to_all(tiles, name, split_axis=0, concat_axis=0)]
    another operation x0 -> x2, local copies, waits for them, and re-layouts: none -> 23.9 us  [swap_blocks(): tiles = jnp.stack(jnp.split(x, count, axis=split), axis=0)]
    reshape x0 -> x1, local copies, waits for them, and re-layouts: none -> 18 us  [swap_blocks(): return jnp.concatenate(tiles, axis=join)]
    all_to_all x1 -> x0, other arithmetic: 17 us -> none  [local(): lax.all_to_all(field, 'lat', split_axis=3, concat_axis=0, tiled=True)]
    unnamed x2 -> x1, other arithmetic: 10.2 us -> 0.01 us
    select_n x1 -> x2, other arithmetic: 0.69 us -> 9.85 us  [local(): field = jnp.take(field, lat_order, axis=3)]
where the time goes in v1:
time: 551 us; the launch traced here: 548 us
  waiting for transfers between devices  164 us (30%)
  local copies, waits for them, and re-layouts  154 us (28%)
  blocking collectives  98.3 us (18%)
  matrix products  65 us (12%)
  other arithmetic  59.6 us (11%)
  starting transfers between devices  5.96 us (1%)
    all_to_all x1, waiting for transfers between devices, local(): lax.all_to_all(swap_blocks(field, 'lat', 3, 0), 'lon', split_axis=3, conc...  164 us
    all_to_all x1, blocking collectives, swap_blocks(): tiles = lax.all_to_all(tiles, name, split_axis=0, concat_axis=0)  98.3 us
    gather x1, local copies, waits for them, and re-layouts, local(): field = jnp.take(field, lat_order, axis=3)  38.6 us
    dot_general x1, matrix products, local(): jnp.einsum('srkej,slj->srel', coeffs_new, legendre, precision=lax.Precisi...  36.1 us
    reduce_sum x1, other arithmetic, local(): jnp.einsum('srkej,slj->srel', coeffs_new, legendre, precision=lax.Precisi...  32.2 us
    dot_general x1, matrix products, synthesize(): jnp.einsum('sreq,srl->qel', values, table, precision=lax.Precision.HIGHEST)  28.9 us
    gather x60, local copies, waits for them, and re-layouts  26.4 us
    another operation x2, local copies, waits for them, and re-layouts, swap_blocks(): tiles = jnp.stack(jnp.split(x, count, axis=split), axis=0)  23.9 us
  transfers between devices with their start and end apart: 1, of which 1 were waited for; matrix products, arithmetic and copies ran while one was open for 3% of the time, Pallas kernels for 0%

profile of v1, /device:TPU:0, one launch (start us, length us, event | category | flops | bytes accessed | tf_op | source)
XLA Modules:
  0.0 548.0 jit_solution(2393428800962391764)
XLA Ops:
  2.0 0.8 fusion.20
  3.5 26.4 %while.1 = (s32[]{:T(128)}, f32[3,1280]{1,0:T(4,128)S(1)}, s32[20,2]{0,1:T(2,128)S(1)}, f32[20,3,640]{2,1,0:T(4,128)S(1)}, s32[]{:T(128)}) while((s32[]{:T(128)}, f32[3,1280]{1,0:T(4,128)S(1)}, s32[20,2]{0,1:T(2,128)S(1)}, f32[20,3,640]{2,1,0:T(4,128)S(1)}, s32[]{:T(128)}) %tuple.24), condition=%wide.while_cond, body=%wide.while_body.sunk | while | flops 2 | bytes 20585 | solution.py:22
  4.1 0.7 bitcast_dynamic-update-slice_fusion.2
  5.4 0.7 bitcast_dynamic-update-slice_fusion.2
  6.7 0.7 bitcast_dynamic-update-slice_fusion.2
  8.1 0.7 bitcast_dynamic-update-slice_fusion.2
  9.4 0.7 bitcast_dynamic-update-slice_fusion.2
  10.7 0.7 bitcast_dynamic-update-slice_fusion.2
  12.0 0.7 bitcast_dynamic-update-slice_fusion.2
  23.9 0.7 bitcast_dynamic-update-slice_fusion.2
  30.8 32.2 %fusion.23 = (f32[20,2,50,640]{3,1,2,0:T(2,128)}, f32[20,2,3,50,640]{4,1,3,2,0:T(2,128)}) fusion(bf16[20,2,3,50,640]{4,1,3,2,0:T(2,128)(2,1)} %param.8, f32[20,3,640]{2,1,0:T(4,128)S(1)} %broadcast_multiply_fusion, f32[20,2,3,50,640]{4,1,3,2,0:T(2,128)} %param.7, f32[3]{0:T(128)} %param.10, pred[20,640]{1,0:T(8,128)(4,1)S(1)} %add_compare_fusion), kind=kLoop, calls=%fused_computation.49 | loop fusion | flops 21760000 | bytes 43686412 | tf_op jit(solution)/shard_map/srkej,slj->srel/reduce_sum | solution.py:52
  63.0 36.1 %fusion = f32[20,2,50,640]{3,2,1,0:T(8,128)} fusion(f32[20,640,640]{2,1,0:T(8,128)} %param.9, f32[20,2,50,640]{3,1,2,0:T(2,128)} %get-tuple-element.18), kind=kOutput, calls=%fused_computation.3 | convolution fusion | flops 9830400000 | bytes 43008000 | tf_op jit(solution)/shard_map/srkej,slj->srel/dot_general | solution.py:52
  99.1 15.9 %copy.29 = f32[20,2,50,640]{2,1,3,0:T(2,128)} copy(f32[20,2,50,640]{3,2,1,0:T(8,128)} %fusion) | data formatting | bytes 10240000 | tf_op jit(solution)/shard_map/srkej,slj->srel/dot_general | solution.py:52
  115.0 38.6 %gather_fusion = f32[640,20,2,50]{3,2,1,0:T(2,128)} fusion(f32[20,2,50,640]{2,1,3,0:T(2,128)} %copy.29, s32[1024]{0:T(1024)S(1)} %pad_clamp_fusion), kind=kCustom, calls=%fused_computation | custom fusion | bytes 10242560 | tf_op jit(solution)/shard_map/jit(_take)/gather | solution.py:53
  153.6 9.2 %select_bitcast_fusion = f32[20,2,50,640]{2,1,0,3:T(2,128)S(1)} fusion(f32[640,20,2,50]{3,2,1,0:T(2,128)} %gather_fusion, pred[640]{0:T(1024)(128)(4,1)S(1)} %compare_and_fusion), kind=kLoop, calls=%fused_computation.6 | loop fusion | flops 1280000 | bytes 10240640 | tf_op jit(solution)/shard_map/jit(_take)/select_n | solution.py:53
  162.7 1.3 fusion.19
  164.0 1.3 fusion.18
  165.3 1.3 fusion.17
  166.6 1.3 fusion.16
  167.9 1.3 fusion.15
  169.2 1.4 fusion.14
  170.6 1.3 fusion.13
  171.8 1.3 fusion.12
  173.2 22.6 %copy.30 = f32[8,20,2,50,80]{4,2,3,1,0:T(2,128)} copy(f32[8,20,2,50,80]{3,2,1,4,0:T(2,128)} %fusion.12) | data formatting | bytes 10240000 | tf_op jit(solution)/shard_map/stack | solution.py:12
  195.8 98.3 %all_to_all.23 = f32[8,20,2,50,80]{4,2,3,1,0:T(2,128)} all-to-all(f32[8,20,2,50,80]{4,2,3,1,0:T(2,128)} %copy.30), channel_id=1, replica_groups=mesh['lat'=8,'lon'=4] {'lat'}, dimensions={0} | all-to-all | bytes 10240000 | tf_op jit(solution)/shard_map/all_to_all | solution.py:13
  294.0 18.0 %copy.31 = f32[160,2,50,80]{0,1,2,3:T(2,128)} copy(f32[160,2,50,80]{3,1,2,0:T(2,128)} %bitcast.66) | data formatting | bytes 10240000 | tf_op jit(solution)/shard_map/reshape | solution.py:14
  312.0 6.0 %all-to-all-start.1 = ((f32[160,2,50,80]{0,1,2,3:T(2,128)}), f32[160,2,50,80]{0,1,2,3:T(2,128)}, u32[]{:S(2)}, u32[]{:S(2)}) async-start(f32[160,2,50,80]{0,1,2,3:T(2,128)} %copy.31), calls=%async_computation.1 | async-start | bytes 16384000 | tf_op jit(solution)/shard_map/all_to_all | solution.py:57
  318.2 15.2 %cosine_multiply_fusion = (f32[640,1,1280]{2,0,1:T(8,128)S(1)}, f32[640,1,1280]{2,0,1:T(8,128)}) fusion(s32[640]{0:T(1024)S(1)} %reshape.188, f32[640]{0:T(1024)S(1)} %get-tuple-element.24, f32[640]{0:T(1024)S(1)} %get-tuple-element.25), kind=kLoop, calls=%fused_computation.17 | loop fusion | flops 9011200 | bytes 6561280 | tf_op jit(solution)/shard_map/mul | solution.py:35
  333.4 164.3 %all-to-all-done.1 = f32[160,2,50,80]{0,1,2,3:T(2,128)} async-done(((f32[160,2,50,80]{0,1,2,3:T(2,128)}), f32[160,2,50,80]{0,1,2,3:T(2,128)}, u32[]{:S(2)}, u32[]{:S(2)}) %all-to-all-start.1) | async-done | bytes 5120032 | tf_op jit(solution)/shard_map/all_to_all | solution.py:57
  497.7 11.8 %copy.38 = f32[4,160,2,50,20]{1,0,3,2,4:T(4,128)} copy(f32[4,160,2,50,20]{1,2,3,4,0:T(2,128)} %bitcast.17) | data formatting | bytes 10240000 | tf_op jit(solution)/shard_map/all_to_all | solution.py:57
  509.5 9.6 %reshape.221 = f32[640,2,50,20]{0,2,1,3:T(8,128)} reshape(f32[4,160,2,50,20]{1,0,3,2,4:T(4,128)} %copy.38) | data formatting | bytes 10240000 | tf_op jit(solution)/shard_map/all_to_all | solution.py:57
  519.1 28.9 %fusion.6 = f32[20,50,1280]{2,1,0:T(8,128)} fusion(f32[640,2,50,20]{0,2,1,3:T(8,128)} %reshape.221, f32[640,1,1280]{2,0,1:T(8,128)} %get-tuple-element.23, f32[640,1,1280]{2,0,1:T(8,128)S(1)} %get-tuple-element.22), kind=kOutput, calls=%fused_computation.13 | convolution fusion | flops 19662438400 | bytes 16793600 | tf_op jit(solution)/shard_map/sreq,srl->qel/dot_general | solution.py:39
  (67 shorter events, 23.7 us)
Async XLA Ops:
  312.0 6.0 %copy-start = (s32[640]{0:T(1024)S(1)}, s32[640]{0:T(1024)}, u32[]{:S(2)}) copy-start(s32[640]{0:T(1024)} %param.12) | copy-start | bytes 7684
  312.0 185.7 %all-to-all-start.1 = ((f32[160,2,50,80]{0,1,2,3:T(2,128)}), f32[160,2,50,80]{0,1,2,3:T(2,128)}, u32[]{:S(2)}, u32[]{:S(2)}) async-start(f32[160,2,50,80]{0,1,2,3:T(2,128)} %copy.31), calls=%async_computation.1 | async-start | bytes 16384000 | tf_op jit(solution)/shard_map/all_to_all | solution.py:57
